TPU v7x, 32 devices: a whole 2x2x4 slice. The times are simulated.
32 devices in a mesh: section: 2 (over y), dp: 4 (over x, core), mp: 4 (over z).
Axes of the slice: x: 2, y: 2, z: 4, core: 2. Of those that a mesh axis runs over, the one named last changes fastest.
Arguments:
- patches: bfloat16 [4096, 1280], P(('section', 'dp')), may hold values from -6 to 6
- patch_counts: int32 [16], P(('section', 'dp')), may hold values from 64 to 256, as said below
- dest_rows: int32 [1024], P(('section', 'dp')), may hold values from 0 to 4095, as said below
- qkv_weight: bfloat16 [1280, 3, 1280], P(None, None, 'mp'), may hold values from -1 to 1
- out_weight: bfloat16 [1280, 1280], P('mp'), may hold values from -0.15625 to 0.15625
- attn_gain: bfloat16 [1280], replicated, may hold values from 0.25 to 1.75
- merge_gain: bfloat16 [1280], replicated, may hold values from 0.25 to 1.75
- fc1_weight: bfloat16 [5120, 5120], P('mp', ('section', 'dp')), may hold values from -0.078125 to 0.078125
- fc1_bias: bfloat16 [5120], P(('section', 'dp')), may hold values from -3 to 3
- fc2_weight: bfloat16 [5120, 8192], P(('section', 'dp'), 'mp'), may hold values from -0.078125 to 0.078125
- fc2_bias: bfloat16 [8192], P('mp'), may hold values from -3 to 3
- text_embeds: bfloat16 [4096, 8192], P(('section', 'dp'), 'mp'), may hold values from -6 to 6
- section_hidden: bfloat16 [4096, 8192], P(('section', 'dp'), 'mp'), may hold values from -80 to 80
- llm_gain: bfloat16 [8192], P('mp'), may hold values from 0.25 to 1.75
Outputs:
- sequence_embeds: bfloat16 [4096, 8192], P(('section', 'dp'), 'mp')
- layer_inputs: bfloat16 [4096, 8192], P(('section', 'dp'), 'mp')
Inputs may be any that keep to these rules, and one draw needn't show every extreme that they name: `patch_counts`: multiples of 4; a tile's patches fill the first slots of its block. `dest_rows`: all rows differ. Each group's merged slots form runs of 16 consecutive slots (aligned); a run goes to one sequence slice (row // 512, numbered in section-major order), different runs of a group to different slices. Rows of slots that are not live are never written.
All inputs are finite; a program needn't handle non-finite values.
Results may differ from a plain program's by a relative error of at most 0.0055.
Values may be sent and summed in bfloat16 or wider, within the bound.
A program may use at most 128 MiB of HBM per device.

v0:
```python
import jax
import jax.numpy as jnp
from jax import lax
from jax.sharding import PartitionSpec as P

HEAD_DIM = 80
HID = 8192
vit_eps = 1e-06
llm_eps = 1e-06


def from_behind(value, axis, steps):
    count = lax.axis_size(axis)
    first, last = (max(0, -steps), min(count, count - steps))
    return lax.ppermute(value, axis, [(source, source + steps) for source in range(first, last)])


def layer_norm(values, gain):
    centred = values.astype(jnp.float32)
    centred = centred - jnp.mean(centred, axis=-1, keepdims=True)
    variance = jnp.mean(centred * centred, axis=-1, keepdims=True)
    return centred * lax.rsqrt(variance + vit_eps) * gain.astype(jnp.float32)


def per_device(
    patches,
    patch_counts,
    dest_rows,
    qkv_weight,
    out_weight,
    attn_gain,
    merge_gain,
    fc1_weight,
    fc1_bias,
    fc2_weight,
    fc2_bias,
    text_embeds,
    section_hidden,
    llm_gain,
):
    width = patches.shape[1]
    tile_total = patch_counts.shape[0]
    block_rows = patches.shape[0] // tile_total
    merged_rows = patches.shape[0] // 4
    local_cols = qkv_weight.shape[2]
    local_heads = local_cols // HEAD_DIM
    feature_cols = text_embeds.shape[1]
    seq_rows = text_embeds.shape[0]
    section_count = lax.axis_size("section")
    group_count = section_count * lax.axis_size("dp")
    run_cap = max(2, merged_rows // group_count)
    run_total = merged_rows // run_cap
    normed_in = layer_norm(patches, attn_gain).astype(jnp.bfloat16)
    projections = jnp.dot(
        normed_in, qkv_weight.reshape(width, 3 * local_cols), preferred_element_type=jnp.float32
    ).astype(jnp.bfloat16)
    projections = projections.reshape(tile_total, block_rows, 3, local_heads, HEAD_DIM)
    query_part = projections[:, :, 0]
    key_part = projections[:, :, 1]
    value_part = projections[:, :, 2]
    scores = jnp.einsum(
        "tqhd,tkhd->thqk", query_part, key_part, preferred_element_type=jnp.float32
    ) * HEAD_DIM ** (-0.5)
    key_live = (
        jnp.arange(block_rows, dtype=jnp.int32)[None, None, None, :]
        < patch_counts[:, None, None, None]
    )
    scores = jnp.where(key_live, scores, -1e30)
    weights = jax.nn.softmax(scores, axis=-1).astype(jnp.bfloat16)
    attended = jnp.einsum(
        "thqk,tkhd->tqhd", weights, value_part, preferred_element_type=jnp.float32
    ).astype(jnp.bfloat16)
    attended = attended.reshape(patches.shape[0], local_cols)
    partial_proj = jnp.dot(attended, out_weight, preferred_element_type=jnp.float32)
    position = lax.axis_index("mp")
    own_patch = lax.dynamic_slice_in_dim(
        patches.reshape(merged_rows, 4, width), position, 1, 1
    ).reshape(merged_rows, width)
    own_proj = lax.psum_scatter(
        partial_proj.reshape(merged_rows, 4, width), "mp", scatter_dimension=1, tiled=True
    ).reshape(merged_rows, width)
    block_out = (own_patch.astype(jnp.float32) + own_proj).astype(jnp.bfloat16)
    merge_part = layer_norm(block_out, merge_gain).astype(jnp.bfloat16)
    first_full, second_full, bias_full = (
        lax.all_gather(fc1_weight, "section", axis=1, tiled=True),
        lax.all_gather(fc2_weight, "section", axis=0, tiled=True),
        lax.all_gather(fc1_bias, "section", axis=0, tiled=True),
    )
    first_partial = jnp.dot(
        lax.all_gather(merge_part, "dp", axis=0, tiled=True),
        first_full,
        preferred_element_type=jnp.float32,
    )
    first_total = lax.psum(first_partial, "mp")
    hidden = jax.nn.gelu(first_total + bias_full.astype(jnp.float32), approximate=False).astype(
        jnp.bfloat16
    )
    embed_total = lax.psum_scatter(
        jnp.dot(hidden, second_full, preferred_element_type=jnp.float32).astype(jnp.bfloat16),
        "dp",
        scatter_dimension=0,
        tiled=True,
    ).astype(jnp.float32)
    image_embeds = (embed_total + fc2_bias.astype(jnp.float32)).astype(jnp.bfloat16)
    slot_in_tile = jnp.arange(merged_rows, dtype=jnp.int32) % (block_rows // 4)
    tile_counts = jnp.repeat(patch_counts, block_rows // 4, total_repeat_length=merged_rows)
    live = slot_in_tile * 4 < tile_counts
    receiver = dest_rows // seq_rows
    run_target = receiver.reshape(run_total, run_cap)[:, 0]
    place = jnp.where(live, dest_rows % seq_rows, seq_rows)
    send_rows = (
        jnp.zeros((group_count, run_cap, feature_cols), jnp.bfloat16)
        .at[run_target]
        .set(image_embeds.reshape(run_total, run_cap, feature_cols))
    )
    send_place = (
        jnp.full((group_count, run_cap), seq_rows, jnp.int32)
        .at[run_target]
        .set(place.reshape(run_total, run_cap))
    )
    got_rows, got_place = (
        lax.all_to_all(send_rows, ("section", "dp"), split_axis=0, concat_axis=0, tiled=True),
        lax.all_to_all(send_place, ("section", "dp"), split_axis=0, concat_axis=0, tiled=True),
    )
    sequence_embeds = text_embeds.at[got_place.reshape(-1)].set(
        got_rows.reshape(-1, feature_cols), mode="drop"
    )
    incoming = from_behind(section_hidden, "section", 1)
    entering = jnp.where(lax.axis_index("section") == 0, sequence_embeds, incoming).astype(
        jnp.float32
    )
    row_total = lax.psum(jnp.sum(entering * entering, axis=1), "mp")
    layer_inputs = (
        entering * lax.rsqrt(row_total / HID + llm_eps)[:, None] * llm_gain.astype(jnp.float32)
    ).astype(jnp.bfloat16)
    return (sequence_embeds, layer_inputs)


def solution(mesh):
    in_specs = (
        P(("section", "dp"), None),
        P(("section", "dp")),
        P(("section", "dp")),
        P(None, None, "mp"),
        P("mp", None),
        P(),
        P(),
        P("mp", ("section", "dp")),
        P(("section", "dp")),
        P(("section", "dp"), "mp"),
        P("mp"),
        P(("section", "dp"), "mp"),
        P(("section", "dp"), "mp"),
        P("mp"),
    )
    out_specs = (P(("section", "dp"), "mp"), P(("section", "dp"), "mp"))
    return jax.shard_map(
        per_device, mesh=mesh, in_specs=in_specs, out_specs=out_specs, check_vma=False
    )
```

profile of v0, /device:TPU:0, one launch (start us, length us, event | category | flops | bytes accessed | tf_op | source)
XLA Modules:
  0.0 317.5 jit_solution(10290408837068384715)
XLA Ops:
  8.1 3.3 %copy.70 = bf16[512,2048]{1,0:T(8,128)(2,1)} copy(bf16[512,2048]{1,0:T(8,128)(2,1)} %param.27) | data formatting | bytes 4194304
  11.4 0.2 convert_reduce_fusion
  11.7 0.5 fusion.6
  12.2 2.6 convolution_convert_fusion.1
  14.8 2.5 reshape.162
  17.3 1.6 fusion.107
  18.9 3.3 %fusion.109 = (f32[2,4,256]{2,1,0:T(4,128)S(1)}, f32[2,4,256,256]{2,3,1,0:T(8,128)}) fusion(pred[2,256]{1,0:T(4,128)(4,1)S(1)} %iota_compare_fusion, bf16[2,256,1,4,80]{1,0,4,3,2:T(2,128)(2,1)} %get-tuple-element.18, bf16[2,256,1,4,80]{1,0,4,3,2:T(2,128)(2,1)} %get-tuple-element.17), kind=kOutput, calls=%fused_computation.154 | convolution fusion | flops 85983488 | bytes 2761216 | tf_op jit(solution)/shard_map/sub | solution.py:69
  22.2 1.9 fusion.56
  24.1 0.3 copy.33
  24.4 0.5 dot_general.23
  24.9 3.5 %fusion.60 = f32[128,4,1280]{2,0,1:T(8,128)} fusion(bf16[320,1280]{1,0:T(8,128)(2,1)} %param.20, bf16[128,4,320]{2,1,0:T(4,128)(2,1)S(1)} %dot_general.23), kind=kOutput, calls=%fused_computation.82 | convolution fusion | flops 419430400 | bytes 3768320 | tf_op jit(solution)/shard_map/dot_general | solution.py:74
  28.5 0.5 all-gather.7.cloned.1.call-update
  29.1 3.5 %reshape.160 = bf16[128,4,1280]{2,1,0:T(4,128)(2,1)} reshape(bf16[512,1280]{1,0:T(8,128)(2,1)} %param.16) | data formatting | bytes 2621440 | tf_op jit(solution)/shard_map/reshape | solution.py:77
  32.6 2.0 constant_dynamic-slice_fusion
  34.6 49.0 %reduce-scatter.3.cloned.1.call-done = f32[128,1,1280]{2,0,1:T(8,128)} async-done(((f32[128,4,1280]{2,0,1:T(8,128)}), f32[128,1,1280]{2,0,1:T(8,128)}) %reduce-scatter.3.cloned.1.call-update) | async-done | bytes 655376 | tf_op jit(solution)/shard_map/reduce_scatter | solution.py:79
  83.6 1.2 convert_reduce_fusion.1
  84.8 0.2 fusion.65
  85.1 1.0 fusion.67
  86.1 0.5 all-gather.9.cloned.1.call-update
  86.7 17.1 %all-gather.5.cloned.1.call-done = bf16[512,1280]{1,0:T(8,128)(2,1)} async-done(((bf16[128,1280]{1,0:T(8,128)(2,1)}), bf16[512,1280]{1,0:T(8,128)(2,1)}) %all-gather.5.cloned.1.call-update) | async-done | bytes 1310736 | tf_op jit(solution)/shard_map/all_gather | solution.py:90
  103.8 5.8 %fusion.110 = f32[512,1280]{1,0:T(8,128)} fusion(bf16[512,1280]{1,0:T(8,128)(2,1)} %all-gather.5.cloned.1.call-done, bf16[1280,1280]{1,0:T(8,128)(2,1)} %all-gather.7.cloned.1.call-done), kind=kOutput, calls=%fused_computation.155 | convolution fusion | flops 1677721600 | bytes 7208960 | tf_op jit(solution)/shard_map/dot_general | solution.py:89
  109.6 0.6 copy-done.7
  110.2 4.5 %all-gather = bf16[2,1,640]{2,1,0:T(2,128)(2,1)S(1)} all-gather(bf16[1,1,640]{2,1,0:T(2,128)(2,1)S(1)} %reshape.198), channel_id=1, replica_groups=mesh['section'=2,'dp'=4,'mp'=4] {'section'}, dimensions={0}, use_global_device_ids=true | all-gather | bytes 3840 | tf_op jit(solution)/shard_map/all_gather | solution.py:87
  114.8 58.8 %all-gather.9.cloned.1.call-done = bf16[1280,2048]{1,0:T(8,128)(2,1)} async-done(((bf16[640,2048]{1,0:T(8,128)(2,1)}), bf16[1280,2048]{1,0:T(8,128)(2,1)}) %all-gather.9.cloned.1.call-update) | async-done | bytes 5242896 | tf_op jit(solution)/shard_map/all_gather | solution.py:86
  173.6 40.2 %all-reduce.2.cloned.1.call-done = f32[512,1280]{1,0:T(8,128)} async-done(((f32[512,1280]{1,0:T(8,128)}), f32[512,1280]{1,0:T(8,128)}) %all-reduce.2.cloned.1.call-update) | async-done | bytes 2621456 | tf_op jit(solution)/shard_map/psum | solution.py:94
  213.8 12.1 %convolution_convert_fusion = bf16[512,2048]{1,0:T(8,128)(2,1)} fusion(bf16[1280,2048]{1,0:T(8,128)(2,1)} %all-gather.9.cloned.1.call-done, f32[512,1280]{1,0:T(8,128)} %all-reduce.2.cloned.1.call-done, f32[1280]{0:T(1024)S(1)} %reshape.200), kind=kOutput, calls=%fused_computation.14 | convolution fusion | flops 2728656896 | bytes 9966592 | tf_op jit(solution)/shard_map/dot_general | solution.py:99
  225.9 4.7 %collective-permute-start = (bf16[512,2048]{1,0:T(8,128)(2,1)}, bf16[512,2048]{1,0:T(8,128)(2,1)}, u32[]{:S(2)}, u32[]{:S(2)}) collective-permute-start(bf16[512,2048]{1,0:T(8,128)(2,1)} %param.28), channel_id=1, source_target_pairs={{0,16},{1,17},{2,18},{3,19},{4,20},{5,21},{6,22},{7,23},{8,24},{9,... | collective-permute-start | bytes 6291464 | tf_op jit(solution)/shard_map/ppermute | solution.py:15
  230.7 0.6 fusion.108
  231.3 1.3 compare_select_fusion.2
  232.6 0.1 reshape.157
  232.6 0.1 reshape.178
  232.7 0.1 fusion.70
  232.8 1.2 scatter_custom_fusion
  234.0 3.3 %all-to-all-start = ((s32[8,1,16]{2,1,0:T(1,128)}), s32[8,1,16]{2,1,0:T(1,128)S(1)}, u32[]{:S(2)}, u32[]{:S(2)}) async-start(s32[8,1,16]{2,1,0:T(1,128)} %bitcast.3), calls=%async_computation | async-start | bytes 8192 | tf_op jit(solution)/shard_map/all_to_all | solution.py:123
  237.3 19.0 %reduce-scatter.5.cloned.1.call-done = bf16[128,2048]{1,0:T(8,128)(2,1)} async-done(((bf16[512,2048]{1,0:T(8,128)(2,1)}), bf16[128,2048]{1,0:T(8,128)(2,1)}) %reduce-scatter.5.cloned.1.call-update) | async-done | bytes 524304 | tf_op jit(solution)/shard_map/reduce_scatter | solution.py:98
  256.3 1.1 add_convert_fusion
  257.4 0.8 broadcast_in_dim.20
  258.3 2.4 scatter_fusion
  260.7 13.7 %all-to-all-done = s32[8,1,16]{2,1,0:T(1,128)S(1)} async-done(((s32[8,1,16]{2,1,0:T(1,128)}), s32[8,1,16]{2,1,0:T(1,128)S(1)}, u32[]{:S(2)}, u32[]{:S(2)}) %all-to-all-start) | async-done | bytes 544 | tf_op jit(solution)/shard_map/all_to_all | solution.py:123
  274.4 4.7 %all-to-all-start.1 = ((bf16[8,16,2048]{2,1,0:T(8,128)(2,1)}), bf16[8,16,2048]{2,1,0:T(8,128)(2,1)S(1)}, u32[]{:S(2)}, u32[]{:S(2)}) async-start(bf16[8,16,2048]{2,1,0:T(8,128)(2,1)} %scatter_fusion), calls=%async_computation.3 | async-start | bytes 1048576 | tf_op jit(solution)/shard_map/all_to_all | solution.py:122
  279.1 0.5 broadcast.190
  279.6 0.6 reduce.10
  280.2 0.1 reshape.159
  280.3 8.5 %all-to-all-done.1 = bf16[8,16,2048]{2,1,0:T(8,128)(2,1)S(1)} async-done(((bf16[8,16,2048]{2,1,0:T(8,128)(2,1)}), bf16[8,16,2048]{2,1,0:T(8,128)(2,1)S(1)}, u32[]{:S(2)}, u32[]{:S(2)}) %all-to-all-start.1) | async-done | bytes 524320 | tf_op jit(solution)/shard_map/all_to_all | solution.py:122
  288.8 4.6 %scatter_fusion.1 = bf16[512,2048]{1,0:T(8,128)(2,1)} fusion(bf16[512,2048]{1,0:T(8,128)(2,1)} %copy.70, s32[128]{0:T(128)S(1)} %fusion.74, bf16[128,2048]{1,0:T(8,128)(2,1)S(1)} %bitcast.61), kind=kCustom, calls=%fused_computation.2 | custom fusion | bytes 1573376 | tf_op jit(solution)/shard_map/scatter | solution.py:125
  293.4 2.3 fusion.1
  295.7 10.0 %psum.15 = f32[512]{0:T(512)S(1)} all-reduce(f32[512]{0:T(512)S(1)} %fusion.1), channel_id=1, replica_groups=mesh['section'=2,'dp'=4,'mp'=4] {'mp'}, use_global_device_ids=true, to_apply=%region_13.14 | all-reduce | flops 512 | bytes 4096 | tf_op jit(solution)/shard_map/psum | solution.py:132
  305.8 4.1 %fusion.3 = bf16[512,2048]{1,0:T(8,128)(2,1)} fusion(f32[2048]{0:T(1024)S(1)} %convert_element_type.88, f32[512]{0:T(512)S(1)} %add_rsqrt_fusion, bf16[512,2048]{1,0:T(8,128)(2,1)} %scatter_fusion.1, bf16[512,2048]{1,0:T(8,128)(2,1)} %collective-permute-done, pred[]{:T(512)S(6)} %eq.6), kind=kLoop, calls=%fused_computation.8 | loop fusion | flops 5242880 | bytes 6301697 | tf_op jit(solution)/shard_map/convert_element_type | solution.py:135
  (47 shorter events, 0.6 us)
Async XLA Ops:
  8.0 4.2 %copy-start = (bf16[1280,3,320]{0,2,1:T(8,128)(2,1)S(1)}, bf16[1280,3,320]{0,2,1:T(8,128)(2,1)}, u32[]{:S(2)}) copy-start(bf16[1280,3,320]{0,2,1:T(8,128)(2,1)} %param.19) | copy-start | bytes 7372804
  8.0 4.1 %copy-start.3 = (bf16[1280]{0:T(1024)(128)(2,1)S(1)}, bf16[1280]{0:T(1024)(128)(2,1)}, u32[]{:S(2)}) copy-start(bf16[1280]{0:T(1024)(128)(2,1)} %param.21) | copy-start | bytes 7684
  8.0 75.6 %reduce-scatter.3.cloned.1.call-start = ((), (), s32[]{:S(2)}) async-start(), calls=%async_computation.4 | async-start | bytes 3276800 | tf_op jit(solution)/shard_map/reduce_scatter | solution.py:79
  8.1 3.3 %copy-start.1 = (bf16[512,1280]{1,0:T(8,128)(2,1)S(1)}, bf16[512,1280]{1,0:T(8,128)(2,1)}, u32[]{:S(2)}) copy-start(bf16[512,1280]{1,0:T(8,128)(2,1)} %param.16) | copy-start | bytes 3932164
  14.8 4.1 %copy-start.8 = (s32[2]{0:T(128)S(1)}, s32[2]{0:T(128)}, u32[]{:S(2)}) copy-start(s32[2]{0:T(128)} %param.17) | copy-start | bytes 28
  18.9 3.4 %copy-start.2 = (bf16[2,256,1,4,80]{1,0,4,3,2:T(2,128)(2,1)S(1)}, bf16[2,256,1,4,80]{1,0,4,3,2:T(2,128)(2,1)}, u32[]{:S(2)}) copy-start(bf16[2,256,1,4,80]{1,0,4,3,2:T(2,128)(2,1)} %get-tuple-element.16) | copy-start | bytes 983044
  28.5 4.1 %copy-start.4 = (bf16[1280]{0:T(1024)(128)(2,1)S(1)}, bf16[1280]{0:T(1024)(128)(2,1)}, u32[]{:S(2)}) copy-start(bf16[1280]{0:T(1024)(128)(2,1)} %param.22) | copy-start | bytes 7684
  28.5 58.3 %all-gather.7.cloned.1.call-start = ((), (), s32[]{:S(2)}) async-start(), calls=%async_computation.6 | async-start | bytes 4915200 | tf_op jit(solution)/shard_map/all_gather | solution.py:85
  29.1 74.7 %all-gather.5.cloned.1.call-start = ((), (), s32[]{:S(2)}) async-start(), calls=%async_computation.5 | async-start | bytes 1638400 | tf_op jit(solution)/shard_map/all_gather | solution.py:90
  86.1 87.6 %all-gather.9.cloned.1.call-start = ((), (), s32[]{:S(2)}) async-start(), calls=%async_computation.8 | async-start | bytes 7864320 | tf_op jit(solution)/shard_map/all_gather | solution.py:86
  86.6 127.2 %all-reduce.2.cloned.1.call-start = ((), (), s32[]{:S(2)}) async-start(), calls=%async_computation.7 | async-start | bytes 5242880 | tf_op jit(solution)/shard_map/psum | solution.py:94
  109.5 0.7 copy-start.7
  109.6 146.7 %reduce-scatter.5.cloned.1.call-start = ((), (), s32[]{:S(2)}) async-start(), calls=%async_computation.9 | async-start | bytes 2621440 | tf_op jit(solution)/shard_map/reduce_scatter | solution.py:98
  114.8 116.5 %copy-start.9 = (s32[128]{0:T(128)S(1)}, s32[128]{0:T(128)}, u32[]{:S(2)}) copy-start(s32[128]{0:T(128)} %param.18) | copy-start | bytes 1540
  114.8 116.5 %copy-start.10 = (pred[128]{0:T(512)(128)(4,1)S(1)}, pred[128]{0:T(512)(128)(4,1)}, u32[]{:S(2)}) copy-start(pred[128]{0:T(512)(128)(4,1)} %constant.224) | copy-start | bytes 388
  114.8 122.4 %copy-start.5 = (bf16[2048]{0:T(1024)(128)(2,1)S(1)}, bf16[2048]{0:T(1024)(128)(2,1)}, u32[]{:S(2)}) copy-start(bf16[2048]{0:T(1024)(128)(2,1)} %param.26) | copy-start | bytes 12292
  225.9 53.1 %copy-start.6 = (bf16[2048]{0:T(1024)(128)(2,1)S(1)}, bf16[2048]{0:T(1024)(128)(2,1)}, u32[]{:S(2)}) copy-start(bf16[2048]{0:T(1024)(128)(2,1)} %param.29) | copy-start | bytes 12292
  225.9 67.4 %collective-permute-start = (bf16[512,2048]{1,0:T(8,128)(2,1)}, bf16[512,2048]{1,0:T(8,128)(2,1)}, u32[]{:S(2)}, u32[]{:S(2)}) collective-permute-start(bf16[512,2048]{1,0:T(8,128)(2,1)} %param.28), channel_id=1, source_target_pairs={{0,16},{1,17},{2,18},{3,19},{4,20},{5,21},{6,22},{7,23},{8,24},{9,... | collective-permute-start | bytes 6291464 | tf_op jit(solution)/shard_map/ppermute | solution.py:15
  234.0 40.4 %all-to-all-start = ((s32[8,1,16]{2,1,0:T(1,128)}), s32[8,1,16]{2,1,0:T(1,128)S(1)}, u32[]{:S(2)}, u32[]{:S(2)}) async-start(s32[8,1,16]{2,1,0:T(1,128)} %bitcast.3), calls=%async_computation | async-start | bytes 8192 | tf_op jit(solution)/shard_map/all_to_all | solution.py:123
  274.4 14.4 %all-to-all-start.1 = ((bf16[8,16,2048]{2,1,0:T(8,128)(2,1)}), bf16[8,16,2048]{2,1,0:T(8,128)(2,1)S(1)}, u32[]{:S(2)}, u32[]{:S(2)}) async-start(bf16[8,16,2048]{2,1,0:T(8,128)(2,1)} %scatter_fusion), calls=%async_computation.3 | async-start | bytes 1048576 | tf_op jit(solution)/shard_map/all_to_all | solution.py:122
Sparse Core Ops, SparseCore 0:
  28.6 54.9 reduce-scatter.2
  109.7 104.0 all-reduce.1
Sparse Core Ops, SparseCore 1:
  30.5 48.9 all-gather.6
  86.2 17.6 all-gather.4
  105.2 68.4 all-gather.8
  226.0 30.2 reduce-scatter.4
where the time goes:
time: 318 us; the launch traced here: 317 us
  waiting for transfers between devices  207 us (65%)
  matrix products  29.1 us (9%)
  local copies, waits for them, and re-layouts  24.8 us (8%)
  between operations  15.9 us (5%)
  blocking collectives  14.6 us (5%)
  starting transfers between devices  12.9 us (4%)
  other arithmetic  12.9 us (4%)
    all_gather x1, waiting for transfers between devices, per_device(): lax.all_gather(fc2_weight, 'section', axis=0, tiled=True)  58.8 us
    reduce_scatter x1, waiting for transfers between devices, per_device(): lax.psum_scatter(partial_proj.reshape(merged_rows, 4, width), 'mp', scatt...  49 us
    psum x1, waiting for transfers between devices, per_device(): first_total = lax.psum(first_partial, 'mp')  40.2 us
    reduce_scatter x1, waiting for transfers between devices, per_device(): lax.psum_scatter(jnp.dot(hidden, second_full, preferred_element_type=jnp....  19 us
    all_gather x1, waiting for transfers between devices, per_device(): lax.all_gather(merge_part, 'dp', axis=0, tiled=True)  17.1 us
    all_to_all x1, waiting for transfers between devices, per_device(): lax.all_to_all(send_place, ('section', 'dp'), split_axis=0, concat_axis=0...  13.7 us
    dot_general x1, matrix products, per_device(): jnp.dot(hidden, second_full, preferred_element_type=jnp.float32)  12.1 us
    psum x1, blocking collectives, per_device(): row_total = lax.psum(jnp.sum(entering * entering, axis=1), 'mp')  10 us
  transfers between devices with their start and end apart: 9, of which 7 were waited for; matrix products, arithmetic and copies ran while one was open for 9% of the time, Pallas kernels for 0%

commit v1 on v0

--- a/solution.py
+++ b/solution.py
@@ -1,3 +1,4 @@
+import functools
 import jax
 import jax.numpy as jnp
 from jax import lax
@@ -7,6 +8,18 @@
 HID = 8192
 vit_eps = 1e-06
 llm_eps = 1e-06
+
+
+def proceed_records(buf, group_axis):
+    world = lax.axis_size(group_axis)
+    kept_arr = buf
+    for p in [hop_no for hop_no in (1, 2, 4, 8, 16) if hop_no < world]:
+        shaped = lax.ppermute(kept_arr, group_axis, [(dev_j, dev_j ^ p) for dev_j in range(world)])
+        kept_arr = kept_arr + shaped
+    return kept_arr
+
+
+plan_the_case = functools.partial(proceed_records, group_axis="mp")
 
 
 def from_behind(value, axis, steps):
@@ -91,7 +104,7 @@
         first_full,
         preferred_element_type=jnp.float32,
     )
-    first_total = lax.psum(first_partial, "mp")
+    first_total = plan_the_case(first_partial)
     hidden = jax.nn.gelu(first_total + bias_full.astype(jnp.float32), approximate=False).astype(
         jnp.bfloat16
     )

time: 318 us -> 395 us (1.24)
  waiting for transfers between devices: 207 us -> 274 us
  other arithmetic: 12.9 us -> 17.3 us
    ppermute x0 -> x2, waiting for transfers between devices: none -> 166 us  [proceed_records(): lax.ppermute(kept_arr, group_axis, [(dev_j, dev_j ^ p) for dev_j in range...]
    all_gather x1, waiting for transfers between devices: 58.8 us -> 0.03 us  [per_device(): lax.all_gather(fc2_weight, 'section', axis=0, tiled=True)]
    psum x1 -> x0, waiting for transfers between devices: 40.2 us -> none  [per_device(): first_total = lax.psum(first_partial, 'mp')]
    add x0 -> x1, other arithmetic: none -> 4.34 us  [proceed_records(): kept_arr = kept_arr + shaped]
  transfers between devices with their start and end apart: 9 -> 10, of which waited for: 7 -> 7; matrix products, arithmetic and copies ran while one was open for 9% -> 7% of each run, Pallas kernels for 0% -> 0%
where the time goes in v1:
time: 395 us; the launch traced here: 394 us
  waiting for transfers between devices  274 us (69%)
  matrix products  29.6 us (7%)
  local copies, waits for them, and re-layouts  24.2 us (6%)
  other arithmetic  17.3 us (4%)
  blocking collectives  17.1 us (4%)
  starting transfers between devices  15.9 us (4%)
  between operations  15.9 us (4%)
    ppermute x2, waiting for transfers between devices, proceed_records(): lax.ppermute(kept_arr, group_axis, [(dev_j, dev_j ^ p) for dev_j in range...  166 us
    reduce_scatter x1, waiting for transfers between devices, per_device(): lax.psum_scatter(partial_proj.reshape(merged_rows, 4, width), 'mp', scatt...  49 us
    reduce_scatter x1, waiting for transfers between devices, per_device(): lax.psum_scatter(jnp.dot(hidden, second_full, preferred_element_type=jnp....  19.8 us
    all_gather x1, waiting for transfers between devices, per_device(): lax.all_gather(merge_part, 'dp', axis=0, tiled=True)  17.6 us
    dot_general x1, matrix products, per_device(): jnp.dot(hidden, second_full, preferred_element_type=jnp.float32)  12.6 us
    psum x1, blocking collectives, per_device(): row_total = lax.psum(jnp.sum(entering * entering, axis=1), 'mp')  12.6 us
    all_to_all x1, waiting for transfers between devices, per_device(): lax.all_to_all(send_place, ('section', 'dp'), split_axis=0, concat_axis=0...  12.3 us
    all_to_all x1, waiting for transfers between devices, per_device(): lax.all_to_all(send_rows, ('section', 'dp'), split_axis=0, concat_axis=0,...  8.45 us
  transfers between devices with their start and end apart: 10, of which 7 were waited for; matrix products, arithmetic and copies ran while one was open for 7% of the time, Pallas kernels for 0%

profile of v1, /device:TPU:0, one launch (start us, length us, event | category | flops | bytes accessed | tf_op | source)
XLA Modules:
  0.0 394.0 jit_solution(4654952679062901406)
XLA Ops:
  8.1 3.3 copy.69
  11.4 0.2 convert_reduce_fusion
  11.7 0.5 fusion.6
  12.2 2.6 convolution_convert_fusion.1
  14.8 2.5 reshape.162
  17.3 1.6 fusion.107
  18.9 3.3 fusion.109
  22.2 1.9 fusion.56
  24.1 0.3 copy.33
  24.4 0.5 dot_general.23
  24.9 3.5 fusion.60
  28.6 0.5 all-gather.7.cloned.1.call-update
  29.1 3.5 reshape.160
  32.6 2.0 constant_dynamic-slice_fusion
  34.6 49.0 %reduce-scatter.3.cloned.1.call-done = f32[128,1,1280]{2,0,1:T(8,128)} async-done(((f32[128,4,1280]{2,0,1:T(8,128)}), f32[128,1,1280]{2,0,1:T(8,128)}) %reduce-scatter.3.cloned.1.call-update) | async-done | bytes 655376 | tf_op jit(solution)/shard_map/reduce_scatter | solution.py:92
  83.6 1.2 convert_reduce_fusion.1
  84.9 0.2 fusion.65
  85.1 1.0 fusion.67
  86.2 17.6 %all-gather.5.cloned.1.call-done = bf16[512,1280]{1,0:T(8,128)(2,1)} async-done(((bf16[128,1280]{1,0:T(8,128)(2,1)}), bf16[512,1280]{1,0:T(8,128)(2,1)}) %all-gather.5.cloned.1.call-update) | async-done | bytes 1310736 | tf_op jit(solution)/shard_map/all_gather | solution.py:103
  103.8 5.7 %fusion.110 = f32[512,1280]{1,0:T(8,128)} fusion(bf16[512,1280]{1,0:T(8,128)(2,1)} %all-gather.5.cloned.1.call-done, bf16[1280,1280]{1,0:T(8,128)(2,1)} %all-gather.7.cloned.1.call-done), kind=kOutput, calls=%fused_computation.156 | convolution fusion | flops 1677721600 | bytes 7208960 | tf_op jit(solution)/shard_map/dot_general | solution.py:102
  109.5 1.5 collective-permute-start
  111.1 57.7 %collective-permute-done = f32[512,1280]{1,0:T(8,128)} collective-permute-done((f32[512,1280]{1,0:T(8,128)}, f32[512,1280]{1,0:T(8,128)}, u32[]{:S(2)}, u32[]{:S(2)}) %collective-permute-start) | collective-permute-done | bytes 2621472 | tf_op jit(solution)/shard_map/ppermute | solution.py:17
  168.8 4.3 %add.114 = f32[512,1280]{1,0:T(8,128)} add(f32[512,1280]{1,0:T(8,128)} %fusion.110, f32[512,1280]{1,0:T(8,128)} %collective-permute-done) | non-fusion elementwise | flops 655360 | bytes 7864320 | tf_op jit(solution)/shard_map/add | solution.py:18
  173.2 2.4 collective-permute-start.1
  175.6 4.5 %all-gather = bf16[2,1,640]{2,1,0:T(2,128)(2,1)S(1)} all-gather(bf16[1,1,640]{2,1,0:T(2,128)(2,1)S(1)} %reshape.198), channel_id=1, replica_groups=mesh['section'=2,'dp'=4,'mp'=4] {'section'}, dimensions={0}, use_global_device_ids=true | all-gather | bytes 3840 | tf_op jit(solution)/shard_map/all_gather | solution.py:100
  180.2 108.5 %collective-permute-done.1 = f32[512,1280]{1,0:T(8,128)} collective-permute-done((f32[512,1280]{1,0:T(8,128)}, f32[512,1280]{1,0:T(8,128)}, u32[]{:S(2)}, u32[]{:S(2)}) %collective-permute-start.1) | collective-permute-done | bytes 2621472 | tf_op jit(solution)/shard_map/ppermute | solution.py:17
  288.7 12.6 %convolution_convert_fusion = bf16[512,2048]{1,0:T(8,128)(2,1)} fusion(bf16[1280,2048]{1,0:T(8,128)(2,1)} %all-gather.9.cloned.1.call-done, f32[512,1280]{1,0:T(8,128)} %add.114, f32[512,1280]{1,0:T(8,128)} %collective-permute-done.1, f32[1280]{0:T(1024)S(1)} %reshape.200), kind=kOutput, calls=%fused_computation.14 | convolution fusion | flops 2729312256 | bytes 12588032 | tf_op jit(solution)/shard_map/dot_general | solution.py:112
  301.3 4.7 %collective-permute-start.2 = (bf16[512,2048]{1,0:T(8,128)(2,1)}, bf16[512,2048]{1,0:T(8,128)(2,1)}, u32[]{:S(2)}, u32[]{:S(2)}) collective-permute-start(bf16[512,2048]{1,0:T(8,128)(2,1)} %param.28), channel_id=1, source_target_pairs={{0,16},{1,17},{2,18},{3,19},{4,20},{5,21},{6,22},{7,23},{8,24},{9,... | collective-permute-start | bytes 6291464 | tf_op jit(solution)/shard_map/ppermute | solution.py:28
  306.1 0.6 fusion.108
  306.7 1.3 compare_select_fusion.2
  308.0 0.1 reshape.157
  308.1 0.1 fusion.70
  308.2 1.2 scatter_custom_fusion
  309.4 3.3 all-to-all-start
  312.7 19.8 %reduce-scatter.5.cloned.1.call-done = bf16[128,2048]{1,0:T(8,128)(2,1)} async-done(((bf16[512,2048]{1,0:T(8,128)(2,1)}), bf16[128,2048]{1,0:T(8,128)(2,1)}) %reduce-scatter.5.cloned.1.call-update) | async-done | bytes 524304 | tf_op jit(solution)/shard_map/reduce_scatter | solution.py:111
  332.5 1.1 add_convert_fusion
  333.7 0.8 broadcast_in_dim.20
  334.5 2.4 scatter_fusion
  336.9 12.3 %all-to-all-done = s32[8,1,16]{2,1,0:T(1,128)S(1)} async-done(((s32[8,1,16]{2,1,0:T(1,128)}), s32[8,1,16]{2,1,0:T(1,128)S(1)}, u32[]{:S(2)}, u32[]{:S(2)}) %all-to-all-start) | async-done | bytes 544 | tf_op jit(solution)/shard_map/all_to_all | solution.py:136
  349.2 3.8 all-to-all-start.1
  353.0 0.5 broadcast.190
  353.5 0.6 reduce.10
  354.1 0.1 reshape.159
  354.2 8.5 %all-to-all-done.1 = bf16[8,16,2048]{2,1,0:T(8,128)(2,1)S(1)} async-done(((bf16[8,16,2048]{2,1,0:T(8,128)(2,1)}), bf16[8,16,2048]{2,1,0:T(8,128)(2,1)S(1)}, u32[]{:S(2)}, u32[]{:S(2)}) %all-to-all-start.1) | async-done | bytes 524320 | tf_op jit(solution)/shard_map/all_to_all | solution.py:135
  362.7 4.6 %scatter_fusion.1 = bf16[512,2048]{1,0:T(8,128)(2,1)} fusion(bf16[512,2048]{1,0:T(8,128)(2,1)} %copy.69, s32[128]{0:T(128)S(1)} %fusion.74, bf16[128,2048]{1,0:T(8,128)(2,1)S(1)} %bitcast.61), kind=kCustom, calls=%fused_computation.2 | custom fusion | bytes 1573376 | tf_op jit(solution)/shard_map/scatter | solution.py:138
  367.3 2.3 fusion.1
  369.6 12.6 %psum.7 = f32[512]{0:T(512)S(1)} all-reduce(f32[512]{0:T(512)S(1)} %fusion.1), channel_id=1, replica_groups=mesh['section'=2,'dp'=4,'mp'=4] {'mp'}, use_global_device_ids=true, to_apply=%region_12.13 | all-reduce | flops 512 | bytes 4096 | tf_op jit(solution)/shard_map/psum | solution.py:145
  382.2 4.1 %fusion.3 = bf16[512,2048]{1,0:T(8,128)(2,1)} fusion(f32[2048]{0:T(1024)S(1)} %convert_element_type.88, f32[512]{0:T(512)S(1)} %add_rsqrt_fusion, bf16[512,2048]{1,0:T(8,128)(2,1)} %scatter_fusion.1, bf16[512,2048]{1,0:T(8,128)(2,1)} %collective-permute-done.2, pred[]{:T(512)S(6)} %eq.6), kind=kLoop, calls=%fused_computation.8 | loop fusion | flops 5242880 | bytes 6301697 | tf_op jit(solution)/shard_map/convert_element_type | solution.py:148
  (49 shorter events, 0.6 us)
Async XLA Ops:
  8.0 4.2 %copy-start = (bf16[1280,3,320]{0,2,1:T(8,128)(2,1)S(1)}, bf16[1280,3,320]{0,2,1:T(8,128)(2,1)}, u32[]{:S(2)}) copy-start(bf16[1280,3,320]{0,2,1:T(8,128)(2,1)} %param.19) | copy-start | bytes 7372804
  8.0 4.1 %copy-start.3 = (bf16[1280]{0:T(1024)(128)(2,1)S(1)}, bf16[1280]{0:T(1024)(128)(2,1)}, u32[]{:S(2)}) copy-start(bf16[1280]{0:T(1024)(128)(2,1)} %param.21) | copy-start | bytes 7684
  8.0 75.6 %reduce-scatter.3.cloned.1.call-start = ((), (), s32[]{:S(2)}) async-start(), calls=%async_computation.4 | async-start | bytes 3276800 | tf_op jit(solution)/shard_map/reduce_scatter | solution.py:92
  8.1 3.3 copy-start.1
  14.8 4.1 %copy-start.8 = (s32[2]{0:T(128)S(1)}, s32[2]{0:T(128)}, u32[]{:S(2)}) copy-start(s32[2]{0:T(128)} %param.17) | copy-start | bytes 28
  18.9 3.4 copy-start.2
  28.5 4.1 %copy-start.4 = (bf16[1280]{0:T(1024)(128)(2,1)S(1)}, bf16[1280]{0:T(1024)(128)(2,1)}, u32[]{:S(2)}) copy-start(bf16[1280]{0:T(1024)(128)(2,1)} %param.22) | copy-start | bytes 7684
  28.5 57.7 %all-gather.7.cloned.1.call-start = ((), (), s32[]{:S(2)}) async-start(), calls=%async_computation.6 | async-start | bytes 4915200 | tf_op jit(solution)/shard_map/all_gather | solution.py:98
  29.1 74.7 %all-gather.5.cloned.1.call-start = ((), (), s32[]{:S(2)}) async-start(), calls=%async_computation.5 | async-start | bytes 1638400 | tf_op jit(solution)/shard_map/all_gather | solution.py:103
  86.1 94.1 %all-gather.9.cloned.1.call-start = ((), (), s32[]{:S(2)}) async-start(), calls=%async_computation.7 | async-start | bytes 7864320 | tf_op jit(solution)/shard_map/all_gather | solution.py:99
  109.5 59.3 %collective-permute-start = (f32[512,1280]{1,0:T(8,128)}, f32[512,1280]{1,0:T(8,128)}, u32[]{:S(2)}, u32[]{:S(2)}) collective-permute-start(f32[512,1280]{1,0:T(8,128)} %fusion.110), channel_id=1, source_target_pairs={{0,1},{1,0},{2,3},{3,2},{4,5},{5,4},{6,7},{7,6},{8,9},{9,8},{10,11... | collective-permute-start | bytes 7864328 | tf_op jit(solution)/shard_map/ppermute | solution.py:17
  111.0 64.6 %copy-start.7 = (bf16[640]{0:T(1024)(128)(2,1)S(1)}, bf16[640]{0:T(1024)(128)(2,1)}, u32[]{:S(2)}) copy-start(bf16[640]{0:T(1024)(128)(2,1)} %param.24) | copy-start | bytes 3844
  111.0 221.5 %reduce-scatter.5.cloned.1.call-start = ((), (), s32[]{:S(2)}) async-start(), calls=%async_computation.8 | async-start | bytes 2621440 | tf_op jit(solution)/shard_map/reduce_scatter | solution.py:111
  173.2 115.5 %collective-permute-start.1 = (f32[512,1280]{1,0:T(8,128)}, f32[512,1280]{1,0:T(8,128)}, u32[]{:S(2)}, u32[]{:S(2)}) collective-permute-start(f32[512,1280]{1,0:T(8,128)} %add.114), channel_id=1, source_target_pairs={{0,2},{1,3},{2,0},{3,1},{4,6},{5,7},{6,4},{7,5},{8,10},{9,11},{10,... | collective-permute-start | bytes 7864328 | tf_op jit(solution)/shard_map/ppermute | solution.py:17
  180.2 126.5 %copy-start.9 = (s32[128]{0:T(128)S(1)}, s32[128]{0:T(128)}, u32[]{:S(2)}) copy-start(s32[128]{0:T(128)} %param.18) | copy-start | bytes 1540
  180.2 126.5 %copy-start.10 = (pred[128]{0:T(512)(128)(4,1)S(1)}, pred[128]{0:T(512)(128)(4,1)}, u32[]{:S(2)}) copy-start(pred[128]{0:T(512)(128)(4,1)} %constant.224) | copy-start | bytes 388
  180.2 132.5 %copy-start.5 = (bf16[2048]{0:T(1024)(128)(2,1)S(1)}, bf16[2048]{0:T(1024)(128)(2,1)}, u32[]{:S(2)}) copy-start(bf16[2048]{0:T(1024)(128)(2,1)} %param.26) | copy-start | bytes 12292
  301.3 51.6 %copy-start.6 = (bf16[2048]{0:T(1024)(128)(2,1)S(1)}, bf16[2048]{0:T(1024)(128)(2,1)}, u32[]{:S(2)}) copy-start(bf16[2048]{0:T(1024)(128)(2,1)} %param.29) | copy-start | bytes 12292
  301.3 65.9 %collective-permute-start.2 = (bf16[512,2048]{1,0:T(8,128)(2,1)}, bf16[512,2048]{1,0:T(8,128)(2,1)}, u32[]{:S(2)}, u32[]{:S(2)}) collective-permute-start(bf16[512,2048]{1,0:T(8,128)(2,1)} %param.28), channel_id=1, source_target_pairs={{0,16},{1,17},{2,18},{3,19},{4,20},{5,21},{6,22},{7,23},{8,24},{9,... | collective-permute-start | bytes 6291464 | tf_op jit(solution)/shard_map/ppermute | solution.py:28
  309.4 39.8 %all-to-all-start = ((s32[8,1,16]{2,1,0:T(1,128)}), s32[8,1,16]{2,1,0:T(1,128)S(1)}, u32[]{:S(2)}, u32[]{:S(2)}) async-start(s32[8,1,16]{2,1,0:T(1,128)} %bitcast.3), calls=%async_computation | async-start | bytes 8192 | tf_op jit(solution)/shard_map/all_to_all | solution.py:136
  349.2 13.5 %all-to-all-start.1 = ((bf16[8,16,2048]{2,1,0:T(8,128)(2,1)}), bf16[8,16,2048]{2,1,0:T(8,128)(2,1)S(1)}, u32[]{:S(2)}, u32[]{:S(2)}) async-start(bf16[8,16,2048]{2,1,0:T(8,128)(2,1)} %scatter_fusion), calls=%async_computation.3 | async-start | bytes 1048576 | tf_op jit(solution)/shard_map/all_to_all | solution.py:135
Sparse Core Ops, SparseCore 0:
  28.6 54.9 reduce-scatter.2
Sparse Core Ops, SparseCore 1:
  30.5 48.9 all-gather.6
  86.2 17.6 all-gather.4
  111.1 67.5 all-gather.8
  301.4 31.0 reduce-scatter.4
